TPU v7x, 8 devices: a whole 2x2x1 slice. The times are simulated.
8 devices in a mesh: dp: 1 (over z), row: 2 (over y), co: 2 (over x), ci: 2 (over core).
Axes of the slice: x: 2, y: 2, z: 1, core: 2. Of those that a mesh axis runs over, the one named last changes fastest.
Arguments:
- x_in: bfloat16 [8192, 3072], P(('dp', 'row'), ('co', 'ci'))
- w_up: bfloat16 [3072, 8192], P('row', ('co', 'ci'))
- w_down: bfloat16 [8192, 3072], P('row', ('co', 'ci'))
Outputs:
- output: bfloat16 [8192, 3072], P(('dp', 'row'), ('co', 'ci'))
All inputs are finite; a program needn't handle non-finite values.
Results may differ from a plain program's by a relative error of at most 0.001.
Values are sent between devices in bfloat16 or wider.
A program may use at most 1 GiB of HBM per device.

v0:
```python
import jax
import jax.numpy as jnp
from jax import lax
from jax.sharding import PartitionSpec as P, NamedSharding

ROW_AXES = ("dp", "row")
COL_AXES = ("co", "ci")


def solution(mesh):
    def local_mlp(x_blk, w_up_blk, w_down_blk):
        x_rows = lax.all_gather(x_blk, COL_AXES, axis=1, tiled=True)
        w_up_cols = lax.all_gather(w_up_blk, "row", axis=0, tiled=True)
        pre_act = jnp.dot(x_rows, w_up_cols, preferred_element_type=jnp.float32)
        hidden = jax.nn.gelu(pre_act, approximate=True).astype(jnp.bfloat16)
        h_rows = lax.all_gather(hidden, COL_AXES, axis=1, tiled=True)
        w_down_cols = lax.all_gather(w_down_blk, "row", axis=0, tiled=True)
        return jnp.dot(h_rows, w_down_cols, preferred_element_type=jnp.float32).astype(jnp.bfloat16)

    act_spec = P(ROW_AXES, COL_AXES)
    wgt_spec = P("row", COL_AXES)
    return jax.shard_map(local_mlp, mesh=mesh, in_specs=(act_spec, wgt_spec, wgt_spec), out_specs=act_spec, check_vma=False)
```

profile of v0, /device:TPU:0, one launch (start us, length us, event | category | flops | bytes accessed | tf_op | source)
XLA Modules:
  0.0 927.5 jit_solution(2053541969706906023)
XLA Ops:
  6.5 0.0 all-gather.7.cloned.1.call-start
  6.5 0.7 all-gather.7.cloned.1.call-update
  7.3 0.0 all-gather.5.cloned.1.call-start
  7.3 0.7 all-gather.5.cloned.1.call-update
  8.0 0.0 all-gather.11.cloned.1.call-start
  8.1 0.7 all-gather.11.cloned.1.call-update
  8.7 0.0 all-gather.9.cloned.1.call-start
  8.8 153.5 %all-gather.7.cloned.1.call-done = bf16[3072,2048]{1,0:T(8,128)(2,1)} async-done(((bf16[1536,2048]{1,0:T(8,128)(2,1)}), bf16[3072,2048]{1,0:T(8,128)(2,1)}) %all-gather.7.cloned.1.call-update) | async-done | bytes 12582928 | tf_op jit(solution)/shard_map/all_gather | solution.py:13
  162.3 154.4 %all-gather.5.cloned.1.call-done = bf16[4096,3072]{1,0:T(8,128)(2,1)} async-done(((bf16[4096,768]{1,0:T(8,128)(2,1)}), bf16[4096,3072]{1,0:T(8,128)(2,1)}) %all-gather.5.cloned.1.call-update) | async-done | bytes 25165840 | tf_op jit(solution)/shard_map/all_gather | solution.py:12
  316.7 66.4 %fusion.7 = bf16[4096,2048]{1,0:T(8,128)(2,1)} fusion(bf16[4096,3072]{1,0:T(8,128)(2,1)} %all-gather.5.cloned.1.call-done, bf16[3072,2048]{1,0:T(8,128)(2,1)} %all-gather.7.cloned.1.call-done), kind=kOutput, calls=%fused_computation.8 | convolution fusion | flops 51615105024 | bytes 54525952 | tf_op jit(solution)/shard_map/dot_general | solution.py:14
  383.1 0.0 all-gather.9.cloned.1.call-update
  383.2 85.7 %all-gather.11.cloned.1.call-done = bf16[8192,768]{1,0:T(8,128)(2,1)} async-done(((bf16[4096,768]{1,0:T(8,128)(2,1)}), bf16[8192,768]{1,0:T(8,128)(2,1)}) %all-gather.11.cloned.1.call-update) | async-done | bytes 12582928 | tf_op jit(solution)/shard_map/all_gather | solution.py:17
  468.8 391.1 %all-gather.9.cloned.1.call-done = bf16[4096,8192]{1,0:T(8,128)(2,1)} async-done(((bf16[4096,2048]{1,0:T(8,128)(2,1)}), bf16[4096,8192]{1,0:T(8,128)(2,1)}) %all-gather.9.cloned.1.call-update) | async-done | bytes 67108880 | tf_op jit(solution)/shard_map/all_gather | solution.py:16
  859.9 61.1 %convolution_convert_fusion = bf16[4096,768]{1,0:T(8,128)(2,1)} fusion(bf16[4096,8192]{1,0:T(8,128)(2,1)} %all-gather.9.cloned.1.call-done, bf16[8192,768]{1,0:T(8,128)(2,1)} %all-gather.11.cloned.1.call-done), kind=kOutput, calls=%fused_computation.9 | convolution fusion | flops 51542753280 | bytes 85983232 | tf_op jit(solution)/shard_map/dot_general | solution.py:18
Async XLA Ops:
  6.5 155.7 %all-gather.7.cloned.1.call-start = ((), (), s32[]{:S(2)}) async-start(), calls=%async_computation.1 | async-start | bytes 18874368 | tf_op jit(solution)/shard_map/all_gather | solution.py:13
  7.3 309.4 %all-gather.5.cloned.1.call-start = ((), (), s32[]{:S(2)}) async-start(), calls=%async_computation | async-start | bytes 31457280 | tf_op jit(solution)/shard_map/all_gather | solution.py:12
  8.0 460.8 %all-gather.11.cloned.1.call-start = ((), (), s32[]{:S(2)}) async-start(), calls=%async_computation.3 | async-start | bytes 18874368 | tf_op jit(solution)/shard_map/all_gather | solution.py:17
  8.7 851.2 %all-gather.9.cloned.1.call-start = ((), (), s32[]{:S(2)}) async-start(), calls=%async_computation.2 | async-start | bytes 83886080 | tf_op jit(solution)/shard_map/all_gather | solution.py:16
Sparse Core Ops, SparseCore 0:
  8.9 153.3 all-gather.6
  163.8 152.8 all-gather.4
  318.2 150.5 all-gather.10
  470.2 389.6 all-gather.8
where the time goes:
time: 928 us
  waiting for transfers between devices  787 us (85%)
  matrix products  128 us (14%)
  between operations  13.1 us (1%)
    all_gather x1, waiting for transfers between devices, local_mlp(): h_rows = lax.all_gather(hidden, COL_AXES, axis=1, tiled=True)  391 us
    all_gather x1, waiting for transfers between devices, local_mlp(): x_rows = lax.all_gather(x_blk, COL_AXES, axis=1, tiled=True)  154 us
    all_gather x1, waiting for transfers between devices, local_mlp(): w_up_cols = lax.all_gather(w_up_blk, 'row', axis=0, tiled=True)  153 us
    all_gather x1, waiting for transfers between devices, local_mlp(): w_down_cols = lax.all_gather(w_down_blk, 'row', axis=0, tiled=True)  85.7 us
    dot_general x1, matrix products, local_mlp(): pre_act = jnp.dot(x_rows, w_up_cols, preferred_element_type=jnp.float32)  66.4 us
    dot_general x1, matrix products, local_mlp(): jnp.dot(h_rows, w_down_cols, preferred_element_type=jnp.float32)  61.1 us
  transfers between devices with their start and end apart: 4, of which 4 were waited for; matrix products, arithmetic and copies ran while one was open for 7% of the time, Pallas kernels for 0%

commit v1 on v0

v1 whole, which is shorter than its diff:
```python
import functools

import jax
import jax.numpy as jnp
from jax import lax
from jax.experimental import pallas as pl
from jax.experimental.pallas import tpu as pltpu
from jax.sharding import PartitionSpec as P

ROW_AXES = ("dp", "row")
COL_AXES = ("co", "ci")
MESH = pl.DeviceIdType.MESH
BF = jnp.bfloat16

W = 256
TT = 512

ITEMS = (
    (0, 0), (0, 1), (0, 2), (0, 3), (0, 4), (1, 4), (1, 0), (0, 5),
    (1, 5), (1, 1), (0, 6), (1, 6), (1, 2), (0, 7), (1, 7), (1, 3),
)
AHEAD = (1, 2, 3, 4, 6, 9, 12, 15)
SERVE = {
    2: ("D4", "Y4"),
    3: ("D5", "V4"),
    5: ("D0", "Y5", "B4", "A0"),
    7: ("D6", "V5"),
    8: ("D1", "Y6", "B5", "A1"),
    10: ("D7", "V6"),
    11: ("D2", "Y7", "B6", "A2"),
    13: ("D3", "V7"),
    14: ("B7", "A3"),
}


def kernel(x_in, w1, w2, y_out, ws, wy_o, wy_s, wx_o, wx_s, wd_o, wd_s, w2s, w2y_o, w2y_s,
           xs, acc, w1b, w2b, st_o, st_s, send, recv, lsem, osem):
    dp, y, x, c = (lax.axis_index(a) for a in ("dp", "row", "co", "ci"))
    tok = x_in.shape[0] // 2
    dh = w1.shape[0]
    cols = x_in.shape[1]
    sib, xn, yn = (dp, y, x, 1 - c), (dp, y, 1 - x, c), (dp, 1 - y, x, c)
    xn2 = (dp, y, 1 - x, 1 - c)

    copies = {}

    def add(name, src, dst, dev):
        i = len(copies)
        copies[name] = functools.partial(
            pltpu.make_async_remote_copy,
            src_ref=src, dst_ref=dst, send_sem=send.at[i], recv_sem=recv.at[i],
            device_id=dev, device_id_type=MESH)

    def start(*names):
        for n in names:
            copies[n]().start()

    def got(*names):
        for n in names:
            copies[n]().wait_recv()

    my_cols = pl.ds(pl.multiple_of((x * 2 + c) * cols, 128), cols)
    my_tok = pl.ds(pl.multiple_of(c * tok, TT), tok)
    sib_tok = pl.ds(pl.multiple_of((1 - c) * tok, TT), tok)
    add("Xc", x_in.at[sib_tok], xs.at[:, my_cols], sib)
    add("Xx", x_in.at[my_tok], xs.at[:, my_cols], xn)
    add("Xz", x_in.at[sib_tok], xs.at[:, my_cols], xn2)
    add("ws", w1, ws, sib)
    add("w2s", w2, w2s, sib)
    nk = w1.shape[1] // W
    for k in range(nk):
        part = w1.at[:, pl.ds(k * W, W)]
        rows = pl.ds(k * W, W)
        add(f"Y{k}", part, wy_o.at[k], yn)
        add(f"fY{k}", wy_o.at[k], wy_s.at[k], sib)
        add(f"D{k}", part, wx_o.at[k], xn)
        add(f"fD{k}", wx_o.at[k], wx_s.at[k], sib)
        add(f"V{k}", w2.at[:, rows], w2y_o.at[:, rows], yn)
        add(f"fV{k}", w2y_o.at[:, rows], w2y_s.at[:, rows], sib)
        if k < nk // 2:
            add(f"A{k}", wy_o.at[k], wd_o.at[k], xn)
            add(f"fA{k}", wd_o.at[k], wd_s.at[k], sib)
        else:
            add(f"B{k}", wx_o.at[k], wd_o.at[k], yn)
            add(f"fB{k}", wd_o.at[k], wd_s.at[k], sib)
    nt = tok // TT
    for t in range(nt):
        add(f"O{t}", st_s.at[pl.ds(t * TT, TT)], y_out.at[pl.ds(pl.multiple_of(c * tok + t * TT, TT), TT)], sib)

    def serve(name):
        got(name)
        start("f" + name)
        kind, k = name[0], int(name[1:])
        if kind == "Y" and k < nk // 2:
            start(f"A{k}")
            start(*(("D6", "D1"), ("D7", "D2"), ("D3",), ())[k])
        if kind == "D" and k >= nk // 2:
            start(f"B{k}")
            start(*(("V5", "Y6"), ("V6", "Y7"), ("V7",), ())[k - nk // 2])

    def loads(i):
        far, k = ITEMS[i]
        slot = i % 2
        part = pl.ds(k * W, W)
        if far:
            srcs = (wx_o.at[k], wd_o.at[k], wx_s.at[k], wd_s.at[k])
        else:
            srcs = (w1.at[:, part], wy_o.at[k], ws.at[:, part], wy_s.at[k])
        out = []
        for j, s in enumerate(srcs):
            rows = pl.ds(pl.multiple_of((y if j % 2 == 0 else 1 - y) * dh, 128), dh)
            lanes = pl.ds(pl.multiple_of((c if j < 2 else 1 - c) * W, 128), W)
            out.append((s, w1b.at[slot, rows, lanes], lsem.at[slot, j]))
        near, dist = ([
            (own.at[:, part], w2b.at[slot, :, :, pl.ds(0, cols)], lsem.at[slot, 4]),
            (oth.at[:, part], w2b.at[slot, :, :, pl.ds(cols, cols)], lsem.at[slot, 5]),
        ] for own, oth in ((w2, w2s), (w2y_o, w2y_s)))
        return out, near, dist

    def load(i):
        far, k = ITEMS[i]
        if far:
            got(f"fD{k}", f"fA{k}" if k < nk // 2 else f"fB{k}")
        else:
            got(f"fY{k}", f"fV{k}")
        first, near, dist = loads(i)
        for d in first:
            pltpu.make_async_copy(*d).start()
        local = (x != y) if far else (x == y)

        @pl.when(local)
        def _():
            for d in near:
                pltpu.make_async_copy(*d).start()

        @pl.when(jnp.logical_not(local))
        def _():
            for d in dist:
                pltpu.make_async_copy(*d).start()

    def loaded(i):
        first, near, _ = loads(i)
        for d in first + near:
            pltpu.make_async_copy(*d).wait()

    barrier = pltpu.get_barrier_semaphore()
    for dev in (sib, xn, xn2, yn):
        pl.semaphore_signal(barrier, inc=1, device_id=dev, device_id_type=MESH)
    pl.semaphore_wait(barrier, 4)

    start("Xx", "Y0", "Xz", "V0", "Xc", "ws", "w2s")
    own = pltpu.make_async_copy(x_in.at[my_tok], xs.at[:, my_cols], osem.at[0])
    own.start()
    start("Y1", "V1", "Y2", "V2", "Y3", "V3", "Y4", "V4", "Y5", "D4", "D5", "D0")

    @pl.loop(0, nt)
    def _(t):
        acc[pl.ds(t * TT, TT), :] = jnp.zeros((TT, acc.shape[1]), jnp.float32)

    for k in range(nk // 2):
        serve(f"Y{k}")
        serve(f"V{k}")
    own.wait()
    got("Xc", "Xx", "Xz", "ws", "w2s")

    def out_copy(t):
        rows = pl.ds(pl.multiple_of(c * tok + t * TT, TT), TT)
        return pltpu.make_async_copy(st_o.at[pl.ds(t * TT, TT)], y_out.at[rows], osem.at[1 + t])

    n_items = len(ITEMS)

    @pl.loop(0, n_items)
    def _(i):
        for n in range(n_items):
            @pl.when(i == n)
            def _():
                for name in SERVE.get(n, ()):
                    serve(name)
                if n not in AHEAD:
                    load(n)
                loaded(n)
                if n + 1 in AHEAD:
                    load(n + 1)

        slot = lax.rem(i, 2)

        @pl.loop(0, nt)
        def _(t):
            rows = pl.ds(pl.multiple_of(t * TT, TT), TT)
            p = jnp.dot(xs[rows, :], w1b[slot], preferred_element_type=jnp.float32)
            h = jax.nn.gelu(p, approximate=True).astype(BF)
            v = w2b[slot].reshape(2 * W, 2 * cols)
            acc[rows, :] += jnp.dot(h, v, preferred_element_type=jnp.float32)

    for t in range(nt):
        rows = pl.ds(t * TT, TT)
        st_s[rows, :] = acc[rows, cols:].astype(BF)
        st_o[rows, :] = acc[rows, :cols].astype(BF)
        if t:
            start(f"O{t - 1}")
            out_copy(t - 1).start()
    start(f"O{nt - 1}")
    out_copy(nt - 1).start()
    for t in range(nt):
        out_copy(t).wait()
        got(f"O{t}")
    for cp in copies.values():
        cp().wait_send()


def solution(mesh):
    def local_mlp(x_blk, w1, w2):
        rows, cols = x_blk.shape
        dh, fq = w1.shape
        tok = rows // 2
        nk = fq // W
        w2v = w2.reshape(2, fq, cols)
        land = jax.ShapeDtypeStruct((nk, dh, W), BF)
        down = jax.ShapeDtypeStruct(w2v.shape, BF)
        n_copies = 5 + 8 * nk + tok // TT
        outs = pl.pallas_call(
            kernel,
            out_shape=[jax.ShapeDtypeStruct(x_blk.shape, BF), jax.ShapeDtypeStruct(w1.shape, BF)] + [land] * 6 + [down] * 3,
            in_specs=[pl.BlockSpec(memory_space=pl.ANY)] * 3,
            out_specs=[pl.BlockSpec(memory_space=pl.ANY)] * 11,
            scratch_shapes=[
                pltpu.VMEM((tok, 4 * cols), BF),
                pltpu.VMEM((tok, 2 * cols), jnp.float32),
                pltpu.VMEM((2, 2 * dh, 2 * W), BF),
                pltpu.VMEM((2, 2, W, 2 * cols), BF),
                pltpu.VMEM((tok, cols), BF),
                pltpu.VMEM((tok, cols), BF),
                pltpu.SemaphoreType.DMA((n_copies,)),
                pltpu.SemaphoreType.DMA((n_copies,)),
                pltpu.SemaphoreType.DMA((2, 6)),
                pltpu.SemaphoreType.DMA((1 + tok // TT,)),
            ],
            compiler_params=pltpu.CompilerParams(
                collective_id=0, has_side_effects=True, vmem_limit_bytes=67_000_000),
        )(x_blk, w1, w2v)
        return outs[0]

    act_spec = P(ROW_AXES, COL_AXES)
    wgt_spec = P("row", COL_AXES)
    return jax.shard_map(local_mlp, mesh=mesh, in_specs=(act_spec, wgt_spec, wgt_spec), out_specs=act_spec, check_vma=False)
```

time: 928 us -> 393 us (0.42)
  waiting for transfers between devices: 787 us -> 0 us
  Pallas kernels: 0 us -> 387 us
  matrix products: 128 us -> 0 us
  between operations: 13.1 us -> 0.01 us
    all_gather x4 -> x0, waiting for transfers between devices: 785 us -> none  [the longest x1 391 us: local_mlp(): h_rows = lax.all_gather(hidden, COL_AXES, axis=1, tiled=True)]
    pallas_call x0 -> x1, Pallas kernels: none -> 387 us  [local_mlp(): pl.pallas_call(kernel, out_shape=[jax.ShapeDtypeStruct(x_blk.shape, BF),...]
    dot_general x2 -> x0, matrix products: 128 us -> none  [the longest x1 66.4 us: local_mlp(): pre_act = jnp.dot(x_rows, w_up_cols, preferred_element_type=jnp.float32)]
  transfers between devices with their start and end apart: 4 -> 0, of which waited for: 4 -> 0; matrix products, arithmetic and copies ran while one was open for 7% -> 0% of each run, Pallas kernels for 0% -> 0%
where the time goes in v1:
time: 393 us
  Pallas kernels  387 us (98%)
  local copies, waits for them, and re-layouts  5.89 us (1%)
    pallas_call x1, Pallas kernels, local_mlp(): pl.pallas_call(kernel, out_shape=[jax.ShapeDtypeStruct(x_blk.shape, BF),...  387 us

profile of v1, /device:TPU:0, one launch (start us, length us, event | category | flops | bytes accessed | tf_op | source)
XLA Modules:
  0.0 393.2 jit_solution(3139371024054421084)
XLA Ops:
  0.0 387.3 %shard_map.37 = (bf16[4096,768]{1,0:T(8,128)(2,1)}, bf16[1536,2048]{1,0:T(8,128)(2,1)}, bf16[8,1536,256]{2,1,0:T(8,128)(2,1)}, bf16[8,1536,256]{2,1,0:T(8,128)(2...) custom-call(bf16[4096,768]{1,0:T(8,128)(2,1)} %x_in.1, ...), custom_call_target="tpu_custom_call" | custom-call | tf_op jit(solution)/shard_map/pallas_call | solution.py:221
  387.3 5.9 %copy.5 = bf16[4096,768]{1,0:T(8,128)(2,1)} copy(bf16[4096,768]{1,0:T(8,128)(2,1)} %get-tuple-element.6) | data formatting | bytes 12582912

commit v2 on v0

v2 whole, which is shorter than its diff:
```python
import functools

import jax
import jax.numpy as jnp
from jax import lax
from jax.experimental import pallas as pl
from jax.experimental.pallas import tpu as pltpu
from jax.sharding import PartitionSpec as P

ROW_AXES = ("dp", "row")
COL_AXES = ("co", "ci")
MESH = pl.DeviceIdType.MESH
BF = jnp.bfloat16

W = 256
HW = W // 2
TT = 512

STEPS = (
    ("full", 0, 0), ("full", 0, 1), ("full", 0, 4), ("hid", 0, 7), ("full", 0, 5),
    ("full", 1, 4), ("full", 0, 2), ("full", 1, 5), ("full", 0, 3), ("hid", 0, 6),
    ("full", 1, 1), ("full", 1, 0), ("full", 1, 2), ("part", 1, 7), ("part", 1, 6),
    ("full", 1, 3), ("comp", 1, 0), ("comp", 1, 1), ("comp", 1, 2), ("comp", 1, 3),
)
LINK_X = (
    "Xx0", "Xz0", "Xx1", "Xz1", "Xx2", "Xz2", "Xx3", "Xz3", "A4", "D4", "D5", "A5",
    "D1", "D0", "D2", "D3", "D7", "D6", "P0", "P1", "P2", "P3",
)
LINK_Y = (
    "Y1", "Y0", "V1", "V0", "V3", "Y4", "V4", "V5", "Y7", "Y5", "Y2", "V2",
    "Y3", "Y6", "B1", "B0", "B2", "B3", "Q0", "Q1", "Q2", "Q3",
)
HOOKS = {
    0: ("Y1", "V0", "Y0", "V1", "L0",),
    1: ("L1",),
    4: ("Y4",),
    6: ("V4",),
    8: ("L2",),
    11: ("V5", "Y7",),
    12: ("L3",),
    13: ("Y5",),
    14: ("D4",),
    16: ("A4", "L4", "L5",),
    18: ("Y2",),
    20: ("V3", "D5",),
    22: ("A5",),
    23: ("V2",),
    24: ("L6", "L7",),
    27: ("D1",),
    28: ("Y3", "L8",),
    31: ("Y6",),
    32: ("D0", "L9",),
    35: ("B1", "D2",),
    36: ("L10",),
    42: ("D3", "B0",),
    43: ("L11",),
    47: ("B2", "D7", "L12",),
    51: ("L13",),
    52: ("D6", "L14",),
    53: ("B3",),
    56: ("L15",),
    59: ("Q0",),
    62: ("P0",),
    65: ("Q1",),
    66: ("P1",),
    67: ("P2",),
    68: ("Q2",),
    73: ("P3", "Q3",),
}
NT = 4
N_TILES = NT * len(STEPS)


def tile_of(b):
    return (b % 2, b // 2) if b < 2 * NT else (b // NT, b % NT)


def links_after():
    def wants(n):
        k = int(n[-1])
        return {"A": f"Y{k}", "B": f"D{k}", "P": f"Y{6 + k // 2}"}.get(n[0])

    served, at, res = set(), [0, 0], {}
    events = [None] + [n for b in sorted(HOOKS) for n in HOOKS[b] if n[0] != "L"]
    for e in events:
        served.add(e)
        new = []
        for j, link in enumerate((LINK_X, LINK_Y)):
            while at[j] < len(link) and (wants(link[at[j]]) is None or wants(link[at[j]]) in served):
                new.append(link[at[j]])
                at[j] += 1
        res[e] = tuple(new)
    assert at == [len(LINK_X), len(LINK_Y)]
    return res


NEXT = links_after()


def any_of(i, kind):
    hit = [i == n for n, s in enumerate(STEPS) if s[0] == kind]
    return functools.reduce(jnp.logical_or, hit)


def kernel(x_in, w1, w2, y_out, ws, wy_o, wy_s, wx_o, wx_s, wd_o, wd_s, w2s, w2y_o, w2y_s,
           xs, acc, w1b, w2b, p32, hn, wl, w2c, send, recv, lsem, osem, csem):
    dp, y, x, c = (lax.axis_index(a) for a in ("dp", "row", "co", "ci"))
    tok = x_in.shape[0] // 2
    dh = w1.shape[0]
    cols = x_in.shape[1]
    nk = w1.shape[1] // W
    nt = NT
    assert tok == NT * TT and nk == 8
    sib, xn, yn = (dp, y, x, 1 - c), (dp, y, 1 - x, c), (dp, 1 - y, x, c)
    xn2 = (dp, y, 1 - x, 1 - c)
    same = x == y
    v_here = jnp.where(same, 1, 0)
    v_there = 1 - v_here

    copies = {}

    def add(name, src, dst, dev):
        i = len(copies)
        copies[name] = functools.partial(
            pltpu.make_async_remote_copy,
            src_ref=src, dst_ref=dst, send_sem=send.at[i], recv_sem=recv.at[i],
            device_id=dev, device_id_type=MESH)

    def start(*names):
        for n in names:
            copies[n]().start()

    def got(*names):
        for n in names:
            copies[n]().wait_recv()

    def at(i, n, unit=128):
        return pl.ds(pl.multiple_of(i * n, unit), n)

    my_cols = at(x * 2 + c, cols)
    my_tok, sib_tok = at(c, tok), at(1 - c, tok)
    add("Xc", x_in.at[sib_tok], xs.at[:, my_cols], sib)
    for q in range(NT):
        for name, who, dev in (("Xx", c, xn), ("Xz", 1 - c, xn2)):
            src = x_in.at[pl.ds(pl.multiple_of(who * tok + q * TT, TT), TT)]
            add(f"{name}{q}", src, xs.at[pl.ds(q * TT, TT), my_cols], dev)
    add("ws", w1, ws, sib)
    add("w2s", w2, w2s, sib)
    for k in range(nk):
        part = pl.ds(k * W, W)
        add(f"Y{k}", w1.at[:, part], wy_o.at[k], yn)
        add(f"fY{k}", wy_o.at[k], wy_s.at[k], sib)
        add(f"D{k}", w1.at[:, part], wx_o.at[k], xn)
        add(f"fD{k}", wx_o.at[k], wx_s.at[k], sib)
        if k < 6:
            add(f"V{k}", w2.at[:, part], w2y_o.at[:, part], yn)
            add(f"fV{k}", w2y_o.at[:, part], w2y_s.at[:, part], sib)
            way = ("B", wx_o, yn) if k < 4 else ("A", wy_o, xn)
            add(f"{way[0]}{k}", way[1].at[k], wd_o.at[k], way[2])
            add(f"f{way[0]}{k}", wd_o.at[k], wd_s.at[k], sib)
    for h in range(4):
        k, half = 6 + h // 2, pl.ds((h % 2) * HW, HW)
        rows = pl.ds(k * W + (h % 2) * HW, HW)
        mine = wl.at[h, :, at(c, HW)]
        add(f"P{h}", wy_o.at[k, :, half], mine, xn)
        add(f"fP{h}", mine, mine, sib)
        left, right = pl.ds(0, cols), pl.ds(cols, cols)
        add(f"Q{h}", w2.at[:, rows], w2c.at[h, v_there, :, :, left], yn)
        add(f"fQ{h}", w2c.at[h, v_here, :, :, left], w2c.at[h, v_here, :, :, right], sib)
    o_base = len(copies)

    def out_copies(t):
        rows = pl.ds(pl.multiple_of(t * TT, TT), TT)
        there = pl.ds(pl.multiple_of(c * tok + t * TT, TT), TT)
        return [pltpu.make_async_remote_copy(
            src_ref=hn.at[j, rows], dst_ref=y_out.at[there, pl.ds(j * W, W)],
            send_sem=send.at[o_base + 3 * t + j], recv_sem=recv.at[o_base + 3 * t + j],
            device_id=sib, device_id_type=MESH) for j in range(3)]

    def serve(name):
        got(name)
        start("f" + name)
        start(*NEXT.get(name, ()))

    def w1_loads(i):
        kind, far, k = STEPS[i]
        slot = i % 2
        part = pl.ds(k * W, W)
        if far:
            srcs = (wx_o.at[k], wd_o.at[k], wx_s.at[k], wd_s.at[k])
        else:
            srcs = (w1.at[:, part], wy_o.at[k], ws.at[:, part], wy_s.at[k])
        out = []
        for j, s in enumerate(srcs):
            rows = at(y if j % 2 == 0 else 1 - y, dh)
            who = c if j < 2 else 1 - c
            if kind == "full":
                out.append((s, w1b.at[slot, rows, at(who, W)], lsem.at[slot, j]))
            elif kind == "hid" or j % 2 == 0:
                for b in range(2):
                    lanes = pl.ds(pl.multiple_of(b * W + who * HW, 128), HW)
                    out.append((s.at[:, pl.ds(b * HW, HW)], w1b.at[slot, rows, lanes], lsem.at[slot, 2 * j + b]))
        return out

    def w2_loads(i, own, oth):
        _, far, k = STEPS[i]
        slot, part = i % 2, pl.ds(k * W, W)
        return [(own.at[:, part], w2b.at[slot, :, :, pl.ds(0, cols)], lsem.at[slot, 8]),
                (oth.at[:, part], w2b.at[slot, :, :, pl.ds(cols, cols)], lsem.at[slot, 9])]

    have_v = set()

    def begin(many):
        for d in many:
            pltpu.make_async_copy(*d).start()

    def load(i):
        kind, far, k = STEPS[i]
        if kind == "comp":
            return
        if far:
            got(f"fD{k}")
            if kind == "full":
                got(f"fB{k}" if k < 4 else f"fA{k}")
        else:
            got(f"fY{k}")
        if kind == "full" and k not in have_v:
            have_v.add(k)
            got(f"fV{k}")
        begin(w1_loads(i))
        if kind == "full":
            local = jnp.logical_not(same) if far else same

            @pl.when(local)
            def _():
                begin(w2_loads(i, w2, w2s))

            @pl.when(jnp.logical_not(local))
            def _():
                begin(w2_loads(i, w2y_o, w2y_s))

    def loaded(i):
        kind, _, k = STEPS[i]
        if kind == "comp":
            got(f"fP{k}", f"fQ{k}")
            return
        for d in w1_loads(i) + (w2_loads(i, w2, w2s) if kind == "full" else []):
            pltpu.make_async_copy(*d).wait()

    barrier = pltpu.get_barrier_semaphore()
    for dev in (sib, xn, xn2, yn):
        pl.semaphore_signal(barrier, inc=1, device_id=dev, device_id_type=MESH)
    pl.semaphore_wait(barrier, 4)

    first = NEXT[None]
    start(*first[:1], "Xc", "ws", "w2s", *first[1:])
    own = pltpu.make_async_copy(x_in.at[my_tok], xs.at[:, my_cols], osem)
    own.start()

    keep = []
    for h in range(4):
        rows = pl.ds((6 + h // 2) * W + (h % 2) * HW, HW)
        for j, src in enumerate((w2, w2s)):
            keep.append((src.at[:, rows], w2c.at[h, v_there, :, :, pl.ds(j * cols, cols)], csem.at[h, j]))
    begin(keep[::2])

    @pl.loop(0, nt)
    def _(t):
        acc[pl.ds(t * TT, TT), :] = jnp.zeros((TT, acc.shape[1]), jnp.float32)

    got("ws", "w2s")
    begin(keep[1::2])
    for d in keep:
        pltpu.make_async_copy(*d).wait()
    own.wait()
    got("Xc")

    n_steps = len(STEPS)
    f32 = jnp.float32

    def before(b):
        i, t = tile_of(b)
        for name in HOOKS.get(b, ()):
            if name[0] == "L":
                load(int(name[1:]))
            else:
                serve(name)
        if t == 0:
            loaded(i)
        if i == 0:
            got(f"Xx{t}", f"Xz{t}")

    @pl.loop(0, N_TILES)
    def _(b):
        for g in range(0, N_TILES, 8):
            @pl.when(jnp.logical_and(b >= g, b < g + 8))
            def _():
                for n in range(g, g + 8):
                    if n in HOOKS or tile_of(n)[0] == 0 or tile_of(n)[1] == 0:
                        pl.when(b == n)(functools.partial(before, n))

        early = b < 2 * NT
        i = jnp.where(early, lax.rem(b, 2), b // NT)
        t = jnp.where(early, b // 2, lax.rem(b, NT))
        slot = lax.rem(i, 2)
        rows = at(t, TT, TT)

        @pl.when(any_of(i, "full"))
        def _():
            p = jnp.dot(xs[rows, :], w1b[slot], preferred_element_type=f32)
            h = jax.nn.gelu(p, approximate=True).astype(BF)
            v = w2b[slot].reshape(2 * W, 2 * cols)
            acc[rows, :] += jnp.dot(h, v, preferred_element_type=f32)

        @pl.when(any_of(i, "hid"))
        def _():
            k2 = 2 * (i == STEPS.index(("hid", 0, 7))).astype(jnp.int32)

            p = jnp.dot(xs[rows, :], w1b[slot], preferred_element_type=f32)
            h = jax.nn.gelu(p, approximate=True).astype(BF)
            hn[k2, rows, :] = h[:, :W]
            hn[k2 + 1, rows, :] = h[:, W:]

        @pl.when(any_of(i, "part"))
        def _():
            k2 = 2 * (i == STEPS.index(("part", 1, 7))).astype(jnp.int32)

            p = jnp.dot(xs[rows, at(y, dh)], w1b[slot, at(y, dh), :], preferred_element_type=f32)
            p32[k2, rows, :] = p[:, :W]
            p32[k2 + 1, rows, :] = p[:, W:]

        @pl.when(any_of(i, "comp"))
        def _():
            j = i - (n_steps - 4)

            p = p32[j, rows, :] + jnp.dot(xs[rows, at(1 - y, dh)], wl[j], preferred_element_type=f32)
            h = jax.nn.gelu(p, approximate=True).astype(BF)
            h = jnp.concatenate([hn[j, rows, :], h], axis=1)
            total = acc[rows, :] + jnp.dot(h, w2c[j].reshape(4 * HW, 2 * cols), preferred_element_type=f32)
            acc[rows, :] = total

            @pl.when(j == 3)
            def _():
                y_out[pl.ds(pl.multiple_of(c * tok + t * TT, TT), TT), :] = acc[rows, :cols].astype(BF)
                for q in range(3):
                    hn[q, rows, :] = acc[rows, cols + q * W:cols + (q + 1) * W].astype(BF)

                @pl.when(t > 0)
                def _():
                    for d in out_copies(t - 1):
                        d.start()

    for d in out_copies(nt - 1):
        d.start()
    for cp in copies.values():
        cp().wait_send()
    for t in range(nt):
        for d in out_copies(t):
            d.wait()


def solution(mesh):
    def local_mlp(x_blk, w1, w2):
        rows, cols = x_blk.shape
        dh, fq = w1.shape
        tok = rows // 2
        nk = fq // W
        w2v = w2.reshape(2, fq, cols)
        land = jax.ShapeDtypeStruct((nk, dh, W), BF)
        down = jax.ShapeDtypeStruct(w2v.shape, BF)
        n_copies = 3 + 2 * NT + 4 * nk + 4 * 6 + 16 + 3 * NT
        dma = pltpu.SemaphoreType.DMA
        outs = pl.pallas_call(
            kernel,
            out_shape=[pltpu.VMEM(x_blk.shape, BF), jax.ShapeDtypeStruct(w1.shape, BF)] + [land] * 6 + [down] * 3,
            in_specs=[pl.BlockSpec(memory_space=pl.ANY)] * 3,
            out_specs=[pl.BlockSpec(memory_space=pltpu.VMEM)] + [pl.BlockSpec(memory_space=pl.ANY)] * 10,
            scratch_shapes=[
                pltpu.VMEM((tok, 4 * cols), BF),
                pltpu.VMEM((tok, 2 * cols), jnp.float32),
                pltpu.VMEM((2, 2 * dh, 2 * W), BF),
                pltpu.VMEM((2, 2, W, 2 * cols), BF),
                pltpu.VMEM((4, tok, W), jnp.float32),
                pltpu.VMEM((4, tok, W), BF),
                pltpu.VMEM((4, dh, W), BF),
                pltpu.VMEM((4, 2, 2, HW, 2 * cols), BF),
                dma((n_copies,)), dma((n_copies,)), dma((2, 10)), dma, dma((4, 2)),
            ],
            compiler_params=pltpu.CompilerParams(
                collective_id=0, has_side_effects=True, vmem_limit_bytes=60_700_000),
        )(x_blk, w1, w2v)
        return outs[0]

    act_spec = P(ROW_AXES, COL_AXES)
    wgt_spec = P("row", COL_AXES)
    return jax.shard_map(local_mlp, mesh=mesh, in_specs=(act_spec, wgt_spec, wgt_spec), out_specs=act_spec, check_vma=False)
```

time: 928 us -> 374 us (0.40)
  waiting for transfers between devices: 787 us -> 0 us
  Pallas kernels: 0 us -> 371 us
  matrix products: 128 us -> 0 us
  between operations: 13.1 us -> 0.01 us
    all_gather x4 -> x0, waiting for transfers between devices: 785 us -> none  [the longest x1 391 us: local_mlp(): h_rows = lax.all_gather(hidden, COL_AXES, axis=1, tiled=True)]
    pallas_call x0 -> x1, Pallas kernels: none -> 371 us  [local_mlp(): pl.pallas_call(kernel, out_shape=[pltpu.VMEM(x_blk.shape, BF), jax.ShapeD...]
    dot_general x2 -> x0, matrix products: 128 us -> none  [the longest x1 66.4 us: local_mlp(): pre_act = jnp.dot(x_rows, w_up_cols, preferred_element_type=jnp.float32)]
  transfers between devices with their start and end apart: 4 -> 0, of which waited for: 4 -> 0; matrix products, arithmetic and copies ran while one was open for 7% -> 0% of each run, Pallas kernels for 0% -> 0%
where the time goes in v2:
time: 374 us
  Pallas kernels  371 us (99%)
    pallas_call x1, Pallas kernels, local_mlp(): pl.pallas_call(kernel, out_shape=[pltpu.VMEM(x_blk.shape, BF), jax.ShapeD...  371 us

profile of v2, /device:TPU:0, one launch (start us, length us, event | category | flops | bytes accessed | tf_op | source)
XLA Modules:
  0.0 374.1 jit_solution(13777891465484609691)
XLA Ops:
  0.0 371.4 %shard_map.37 = (bf16[4096,768]{1,0:T(8,128)(2,1)S(1)}, bf16[1536,2048]{1,0:T(8,128)(2,1)}, bf16[8,1536,256]{2,1,0:T(8,128)(2,1)}, bf16[8,1536,256]{2,1,0:T(8,12...) custom-call(bf16[4096,768]{1,0:T(8,128)(2,1)} %x_in.1, ...), custom_call_target="tpu_custom_call" | custom-call | tf_op jit(solution)/shard_map/pallas_call | solution.py:373
  371.4 2.7 copy.5

commit v3 on v2

--- a/solution.py
+++ b/solution.py
@@ -11,10 +11,12 @@
 COL_AXES = ("co", "ci")
 MESH = pl.DeviceIdType.MESH
 BF = jnp.bfloat16
+GELU_A = 0.7978845608028654
 
 W = 256
 HW = W // 2
 TT = 512
+ST = TT // 2
 
 STEPS = (
     ("full", 0, 0), ("full", 0, 1), ("full", 0, 4), ("hid", 0, 7), ("full", 0, 5),
@@ -97,9 +99,14 @@
 NEXT = links_after()
 
 
-def any_of(i, kind):
-    hit = [i == n for n, s in enumerate(STEPS) if s[0] == kind]
-    return functools.reduce(jnp.logical_or, hit)
+def is_kind(i, kind):
+    mask = sum(1 << n for n, s in enumerate(STEPS) if s[0] == kind)
+    return lax.rem(lax.shift_right_logical(jnp.int32(mask), i), 2) == 1
+
+
+def gelu(p):
+    u = p * (GELU_A + (GELU_A * 0.044715) * (p * p))
+    return (0.5 * p) * (1.0 + jnp.tanh(u))
 
 
 def kernel(x_in, w1, w2, y_out, ws, wy_o, wy_s, wx_o, wx_s, wd_o, wd_s, w2s, w2y_o, w2y_s,
@@ -292,12 +299,17 @@
 
     @pl.loop(0, N_TILES)
     def _(b):
-        for g in range(0, N_TILES, 8):
-            @pl.when(jnp.logical_and(b >= g, b < g + 8))
-            def _():
-                for n in range(g, g + 8):
-                    if n in HOOKS or tile_of(n)[0] == 0 or tile_of(n)[1] == 0:
-                        pl.when(b == n)(functools.partial(before, n))
+        def pick(lo, hi):
+            if not any(n in busy for n in range(lo, hi)):
+                return lambda: None
+            if hi - lo == 1:
+                return functools.partial(before, lo)
+            mid = (lo + hi) // 2
+            low, high = pick(lo, mid), pick(mid, hi)
+            return lambda: lax.cond(b < mid, low, high)
+
+        busy = [n for n in range(N_TILES) if n in HOOKS or tile_of(n)[0] == 0 or tile_of(n)[1] == 0]
+        pick(0, N_TILES)()
 
         early = b < 2 * NT
         i = jnp.where(early, lax.rem(b, 2), b // NT)
@@ -305,50 +317,57 @@
         slot = lax.rem(i, 2)
         rows = at(t, TT, TT)
 
-        @pl.when(any_of(i, "full"))
+        subs = [pl.ds(pl.multiple_of(t * TT + q * ST, ST), ST) for q in range(TT // ST)]
+
+        @pl.when(is_kind(i, "full"))
         def _():
-            p = jnp.dot(xs[rows, :], w1b[slot], preferred_element_type=f32)
-            h = jax.nn.gelu(p, approximate=True).astype(BF)
-            v = w2b[slot].reshape(2 * W, 2 * cols)
-            acc[rows, :] += jnp.dot(h, v, preferred_element_type=f32)
-
-        @pl.when(any_of(i, "hid"))
+            ps = [jnp.dot(xs[r, :], w1b[slot], preferred_element_type=f32) for r in subs]
+            for r, p in zip(subs, ps):
+                h = gelu(p).astype(BF)
+                v = w2b[slot].reshape(2 * W, 2 * cols)
+                acc[r, :] += jnp.dot(h, v, preferred_element_type=f32)
+
+        @pl.when(is_kind(i, "hid"))
         def _():
             k2 = 2 * (i == STEPS.index(("hid", 0, 7))).astype(jnp.int32)
-
-            p = jnp.dot(xs[rows, :], w1b[slot], preferred_element_type=f32)
-            h = jax.nn.gelu(p, approximate=True).astype(BF)
-            hn[k2, rows, :] = h[:, :W]
-            hn[k2 + 1, rows, :] = h[:, W:]
-
-        @pl.when(any_of(i, "part"))
+            ps = [jnp.dot(xs[r, :], w1b[slot], preferred_element_type=f32) for r in subs]
+            for r, p in zip(subs, ps):
+                h = gelu(p).astype(BF)
+                hn[k2, r, :] = h[:, :W]
+                hn[k2 + 1, r, :] = h[:, W:]
+
+        @pl.when(is_kind(i, "part"))
         def _():
             k2 = 2 * (i == STEPS.index(("part", 1, 7))).astype(jnp.int32)
-
             p = jnp.dot(xs[rows, at(y, dh)], w1b[slot, at(y, dh), :], preferred_element_type=f32)
             p32[k2, rows, :] = p[:, :W]
             p32[k2 + 1, rows, :] = p[:, W:]
 
-        @pl.when(any_of(i, "comp"))
+        def comp(j):
+            ps = [p32[j, r, :] + jnp.dot(xs[r, at(1 - y, dh)], wl[j], preferred_element_type=f32) for r in subs]
+            for r, p in zip(subs, ps):
+                h = jnp.concatenate([hn[j, r, :], gelu(p).astype(BF)], axis=1)
+                v = w2c[j].reshape(4 * HW, 2 * cols)
+                yield r, acc[r, :] + jnp.dot(h, v, preferred_element_type=f32)
+
+        last = i == n_steps - 1
+
+        @pl.when(jnp.logical_and(is_kind(i, "comp"), jnp.logical_not(last)))
         def _():
-            j = i - (n_steps - 4)
-
-            p = p32[j, rows, :] + jnp.dot(xs[rows, at(1 - y, dh)], wl[j], preferred_element_type=f32)
-            h = jax.nn.gelu(p, approximate=True).astype(BF)
-            h = jnp.concatenate([hn[j, rows, :], h], axis=1)
-            total = acc[rows, :] + jnp.dot(h, w2c[j].reshape(4 * HW, 2 * cols), preferred_element_type=f32)
-            acc[rows, :] = total
-
-            @pl.when(j == 3)
+            for r, total in comp(i - (n_steps - 4)):
+                acc[r, :] = total
+
+        @pl.when(last)
+        def _():
+            for q, (r, total) in enumerate(comp(3)):
+                y_out[pl.ds(pl.multiple_of(c * tok + t * TT + q * ST, ST), ST), :] = total[:, :cols].astype(BF)
+                for m in range(3):
+                    hn[m, r, :] = total[:, cols + m * W:cols + (m + 1) * W].astype(BF)
+
+            @pl.when(t > 0)
             def _():
-                y_out[pl.ds(pl.multiple_of(c * tok + t * TT, TT), TT), :] = acc[rows, :cols].astype(BF)
-                for q in range(3):
-                    hn[q, rows, :] = acc[rows, cols + q * W:cols + (q + 1) * W].astype(BF)
-
-                @pl.when(t > 0)
-                def _():
-                    for d in out_copies(t - 1):
-                        d.start()
+                for d in out_copies(t - 1):
+                    d.start()
 
     for d in out_copies(nt - 1):
         d.start()

time: 374 us -> 366 us (0.979)
  Pallas kernels: 371 us -> 363 us
    pallas_call x1, Pallas kernels: 371 us -> 363 us  [local_mlp(): pl.pallas_call(kernel, out_shape=[pltpu.VMEM(x_blk.shape, BF), jax.ShapeD...]
where the time goes in v3:
time: 366 us
  Pallas kernels  363 us (99%)
    pallas_call x1, Pallas kernels, local_mlp(): pl.pallas_call(kernel, out_shape=[pltpu.VMEM(x_blk.shape, BF), jax.ShapeD...  363 us

profile of v3, /device:TPU:0, one launch (start us, length us, event | category | flops | bytes accessed | tf_op | source)
XLA Modules:
  0.0 365.6 jit_solution(13503079216082828558)
XLA Ops:
  0.0 362.9 %shard_map.37 = (bf16[4096,768]{1,0:T(8,128)(2,1)S(1)}, bf16[1536,2048]{1,0:T(8,128)(2,1)}, bf16[8,1536,256]{2,1,0:T(8,128)(2,1)}, bf16[8,1536,256]{2,1,0:T(8,12...) custom-call(bf16[4096,768]{1,0:T(8,128)(2,1)} %x_in.1, ...), custom_call_target="tpu_custom_call" | custom-call | tf_op jit(solution)/shard_map/pallas_call | solution.py:392
  362.9 2.7 copy.5

commit v4 on v3

--- a/solution.py
+++ b/solution.py
@@ -19,62 +19,81 @@
 ST = TT // 2
 
 STEPS = (
-    ("full", 0, 0), ("full", 0, 1), ("full", 0, 4), ("hid", 0, 7), ("full", 0, 5),
-    ("full", 1, 4), ("full", 0, 2), ("full", 1, 5), ("full", 0, 3), ("hid", 0, 6),
-    ("full", 1, 1), ("full", 1, 0), ("full", 1, 2), ("part", 1, 7), ("part", 1, 6),
-    ("full", 1, 3), ("comp", 1, 0), ("comp", 1, 1), ("comp", 1, 2), ("comp", 1, 3),
+    ("hid", 0, 6, 0, 3), ("hid", 0, 7, 0, 3), ("full", 0, 1, 0, 4), ("full", 0, 5, 0, 3),
+    ("hid", 0, 7, 3, 4), ("full", 0, 3, 0, 4), ("full", 0, 5, 3, 4), ("full", 0, 4, 1, 4),
+    ("hid", 0, 6, 3, 4), ("full", 0, 4, 0, 1), ("full", 1, 5, 0, 4), ("full", 0, 0, 0, 4),
+    ("full", 1, 4, 2, 4), ("full", 1, 4, 0, 1), ("full", 0, 2, 0, 4), ("full", 1, 3, 0, 4),
+    ("full", 1, 4, 1, 2), ("full", 1, 2, 0, 4), ("full", 1, 0, 0, 4), ("part", 1, 6, 0, 4),
+    ("full", 1, 1, 0, 4), ("part", 1, 7, 0, 4), ("comp", 1, 0, 0, 4), ("comp", 1, 1, 0, 4),
+    ("comp", 1, 2, 0, 4), ("last", 1, 3, 0, 4), ("own", 1, 3, 0, 4),
 )
 LINK_X = (
-    "Xx0", "Xz0", "Xx1", "Xz1", "Xx2", "Xz2", "Xx3", "Xz3", "A4", "D4", "D5", "A5",
-    "D1", "D0", "D2", "D3", "D7", "D6", "P0", "P1", "P2", "P3",
+    "Xx1", "Xx2", "Xz0", "Xz2", "Xz1", "Xx0", "Xz3", "D5", "Xx3", "A5", "D4", "D3",
+    "A4", "D2", "D0", "D1", "D6", "P0", "D7", "P1", "P2", "P3",
 )
 LINK_Y = (
-    "Y1", "Y0", "V1", "V0", "V3", "Y4", "V4", "V5", "Y7", "Y5", "Y2", "V2",
-    "Y3", "Y6", "B1", "B0", "B2", "B3", "Q0", "Q1", "Q2", "Q3",
+    "Y6", "V3", "V1", "Y1", "Y5", "Y7", "V5", "Y3", "Y4", "V4", "V0", "Y0",
+    "V2", "Y2", "B3", "B2", "B0", "B1", "Q0", "Q1", "Q2", "Q3",
 )
 HOOKS = {
-    0: ("Y1", "V0", "Y0", "V1", "L0",),
-    1: ("L1",),
-    4: ("Y4",),
-    6: ("V4",),
-    8: ("L2",),
-    11: ("V5", "Y7",),
-    12: ("L3",),
-    13: ("Y5",),
-    14: ("D4",),
-    16: ("A4", "L4", "L5",),
-    18: ("Y2",),
-    20: ("V3", "D5",),
-    22: ("A5",),
-    23: ("V2",),
-    24: ("L6", "L7",),
-    27: ("D1",),
-    28: ("Y3", "L8",),
-    31: ("Y6",),
-    32: ("D0", "L9",),
-    35: ("B1", "D2",),
-    36: ("L10",),
-    42: ("D3", "B0",),
-    43: ("L11",),
-    47: ("B2", "D7", "L12",),
-    51: ("L13",),
-    52: ("D6", "L14",),
-    53: ("B3",),
-    56: ("L15",),
-    59: ("Q0",),
-    62: ("P0",),
-    65: ("Q1",),
-    66: ("P1",),
-    67: ("P2",),
+    0: ("Y7", "Y6", "V1", "Y1", "L0",),
+    1: ("Y5",),
+    2: ("L1",),
+    3: ("L2",),
+    6: ("V5",),
+    7: ("L3",),
+    8: ("Y3",),
+    10: ("Y4",),
+    12: ("V3", "L4",),
+    13: ("L5",),
+    14: ("D5",),
+    15: ("L6",),
+    16: ("V4",),
+    18: ("L7",),
+    19: ("A5",),
+    21: ("V0", "L8",),
+    22: ("Y0", "D4", "L9",),
+    23: ("L10",),
+    27: ("D3", "L11",),
+    28: ("V2", "A4",),
+    30: ("L12",),
+    32: ("L13",),
+    33: ("D2",),
+    34: ("Y2", "L14",),
+    38: ("B3", "L15",),
+    40: ("L16",),
+    41: ("D0",),
+    42: ("B2",),
+    43: ("L17",),
+    44: ("D1",),
+    47: ("B0", "D6", "L18",),
+    51: ("L19",),
+    52: ("B1",),
+    53: ("P0",),
+    54: ("L20",),
+    58: ("D7",),
+    59: ("L21",),
+    60: ("Q0",),
+    62: ("Q1",),
+    64: ("P1",),
     68: ("Q2",),
-    73: ("P3", "Q3",),
+    69: ("P2",),
+    74: ("P3", "Q3",),
 }
 NT = 4
-N_TILES = NT * len(STEPS)
-
-
-def tile_of(b):
-    return (b % 2, b // 2) if b < 2 * NT else (b // NT, b % NT)
+TILES = [(i, t) for i, s in enumerate(STEPS) for t in range(s[3], s[4])]
+N_TILES = len(TILES)
+FIRST = [TILES.index((i, s[3])) for i, s in enumerate(STEPS)]
+NEW_X = [min(b for b in range(N_TILES) if TILES[b][1] == t) for t in range(NT)]
+
+
+def step_and_tile(b):
+    i = off = jnp.int32(0)
+    for n in range(1, len(STEPS)):
+        begun = (b >= FIRST[n]).astype(jnp.int32)
+        i += begun
+        off += begun * ((FIRST[n] - STEPS[n][3]) - (FIRST[n - 1] - STEPS[n - 1][3]))
+    return i, b + STEPS[0][3] - off
 
 
 def links_after():
@@ -100,7 +119,7 @@
 
 
 def is_kind(i, kind):
-    mask = sum(1 << n for n, s in enumerate(STEPS) if s[0] == kind)
+    mask = sum(1 << n for n, s in enumerate(STEPS) if s[:len(kind)] == kind)
     return lax.rem(lax.shift_right_logical(jnp.int32(mask), i), 2) == 1
 
 
@@ -190,7 +209,7 @@
         start(*NEXT.get(name, ()))
 
     def w1_loads(i):
-        kind, far, k = STEPS[i]
+        kind, far, k = STEPS[i][:3]
         slot = i % 2
         part = pl.ds(k * W, W)
         if far:
@@ -210,30 +229,26 @@
         return out
 
     def w2_loads(i, own, oth):
-        _, far, k = STEPS[i]
+        _, far, k = STEPS[i][:3]
         slot, part = i % 2, pl.ds(k * W, W)
         return [(own.at[:, part], w2b.at[slot, :, :, pl.ds(0, cols)], lsem.at[slot, 8]),
                 (oth.at[:, part], w2b.at[slot, :, :, pl.ds(cols, cols)], lsem.at[slot, 9])]
 
-    have_v = set()
+    waited = set()
 
     def begin(many):
         for d in many:
             pltpu.make_async_copy(*d).start()
 
     def load(i):
-        kind, far, k = STEPS[i]
-        if kind == "comp":
+        kind, far, k = STEPS[i][:3]
+        if kind in ("comp", "last", "own"):
             return
-        if far:
-            got(f"fD{k}")
-            if kind == "full":
-                got(f"fB{k}" if k < 4 else f"fA{k}")
-        else:
-            got(f"fY{k}")
-        if kind == "full" and k not in have_v:
-            have_v.add(k)
-            got(f"fV{k}")
+        need = [f"fD{k}" if far else f"fY{k}"]
+        if kind == "full":
+            need += [f"fV{k}"] + ([f"fB{k}" if k < 4 else f"fA{k}"] if far else [])
+        got(*(n for n in need if n not in waited))
+        waited.update(need)
         begin(w1_loads(i))
         if kind == "full":
             local = jnp.logical_not(same) if far else same
@@ -247,9 +262,10 @@
                 begin(w2_loads(i, w2y_o, w2y_s))
 
     def loaded(i):
-        kind, _, k = STEPS[i]
-        if kind == "comp":
+        kind, _, k = STEPS[i][:3]
+        if kind in ("comp", "last"):
             got(f"fP{k}", f"fQ{k}")
+        if kind in ("comp", "last", "own"):
             return
         for d in w1_loads(i) + (w2_loads(i, w2, w2s) if kind == "full" else []):
             pltpu.make_async_copy(*d).wait()
@@ -286,15 +302,15 @@
     f32 = jnp.float32
 
     def before(b):
-        i, t = tile_of(b)
+        i, t = TILES[b]
         for name in HOOKS.get(b, ()):
             if name[0] == "L":
                 load(int(name[1:]))
             else:
                 serve(name)
-        if t == 0:
+        if b in FIRST:
             loaded(i)
-        if i == 0:
+        if b in NEW_X:
             got(f"Xx{t}", f"Xz{t}")
 
     @pl.loop(0, N_TILES)
@@ -308,18 +324,16 @@
             low, high = pick(lo, mid), pick(mid, hi)
             return lambda: lax.cond(b < mid, low, high)
 
-        busy = [n for n in range(N_TILES) if n in HOOKS or tile_of(n)[0] == 0 or tile_of(n)[1] == 0]
+        busy = set(HOOKS) | set(FIRST) | set(NEW_X)
         pick(0, N_TILES)()
 
-        early = b < 2 * NT
-        i = jnp.where(early, lax.rem(b, 2), b // NT)
-        t = jnp.where(early, b // 2, lax.rem(b, NT))
+        i, t = step_and_tile(b)
         slot = lax.rem(i, 2)
         rows = at(t, TT, TT)
 
         subs = [pl.ds(pl.multiple_of(t * TT + q * ST, ST), ST) for q in range(TT // ST)]
 
-        @pl.when(is_kind(i, "full"))
+        @pl.when(is_kind(i, ("full",)))
         def _():
             ps = [jnp.dot(xs[r, :], w1b[slot], preferred_element_type=f32) for r in subs]
             for r, p in zip(subs, ps):
@@ -327,50 +341,61 @@
                 v = w2b[slot].reshape(2 * W, 2 * cols)
                 acc[r, :] += jnp.dot(h, v, preferred_element_type=f32)
 
-        @pl.when(is_kind(i, "hid"))
-        def _():
-            k2 = 2 * (i == STEPS.index(("hid", 0, 7))).astype(jnp.int32)
+        @pl.when(is_kind(i, ("hid",)))
+        def _():
+            k2 = 2 * is_kind(i, ("hid", 0, 7)).astype(jnp.int32)
             ps = [jnp.dot(xs[r, :], w1b[slot], preferred_element_type=f32) for r in subs]
             for r, p in zip(subs, ps):
                 h = gelu(p).astype(BF)
                 hn[k2, r, :] = h[:, :W]
                 hn[k2 + 1, r, :] = h[:, W:]
 
-        @pl.when(is_kind(i, "part"))
-        def _():
-            k2 = 2 * (i == STEPS.index(("part", 1, 7))).astype(jnp.int32)
+        @pl.when(is_kind(i, ("part",)))
+        def _():
+            k2 = 2 * is_kind(i, ("part", 1, 7)).astype(jnp.int32)
             p = jnp.dot(xs[rows, at(y, dh)], w1b[slot, at(y, dh), :], preferred_element_type=f32)
             p32[k2, rows, :] = p[:, :W]
             p32[k2 + 1, rows, :] = p[:, W:]
 
-        def comp(j):
-            ps = [p32[j, r, :] + jnp.dot(xs[r, at(1 - y, dh)], wl[j], preferred_element_type=f32) for r in subs]
-            for r, p in zip(subs, ps):
-                h = jnp.concatenate([hn[j, r, :], gelu(p).astype(BF)], axis=1)
-                v = w2c[j].reshape(4 * HW, 2 * cols)
-                yield r, acc[r, :] + jnp.dot(h, v, preferred_element_type=f32)
-
-        last = i == n_steps - 1
-
-        @pl.when(jnp.logical_and(is_kind(i, "comp"), jnp.logical_not(last)))
-        def _():
-            for r, total in comp(i - (n_steps - 4)):
-                acc[r, :] = total
-
-        @pl.when(last)
-        def _():
-            for q, (r, total) in enumerate(comp(3)):
-                y_out[pl.ds(pl.multiple_of(c * tok + t * TT + q * ST, ST), ST), :] = total[:, :cols].astype(BF)
+        def far_p(j):
+            return [p32[j, r, :] + jnp.dot(xs[r, at(1 - y, dh)], wl[j], preferred_element_type=f32) for r in subs]
+
+        def down(j, half, lo, hi):
+            return w2c[j, half, :, :, lo * cols:hi * cols].reshape(2 * HW, (hi - lo) * cols)
+
+        @pl.when(is_kind(i, ("comp",)))
+        def _():
+            j = i - STEPS.index(("comp", 1, 0, 0, NT))
+            for r, p in zip(subs, far_p(j)):
+                total = acc[r, :] + jnp.dot(hn[j, r, :], down(j, 0, 0, 2), preferred_element_type=f32)
+                acc[r, :] = total + jnp.dot(gelu(p).astype(BF), down(j, 1, 0, 2), preferred_element_type=f32)
+
+        @pl.when(is_kind(i, ("last",)))
+        def _():
+            for r, p in zip(subs, far_p(3)):
+                h = gelu(p).astype(BF)
+                w1b[0, r, :W] = h
+                total = acc[r, cols:] + jnp.dot(hn[3, r, :], down(3, 0, 1, 2), preferred_element_type=f32)
+                total = (total + jnp.dot(h, down(3, 1, 1, 2), preferred_element_type=f32)).astype(BF)
                 for m in range(3):
-                    hn[m, r, :] = total[:, cols + m * W:cols + (m + 1) * W].astype(BF)
+                    hn[m, r, :] = total[:, m * W:(m + 1) * W]
 
             @pl.when(t > 0)
             def _():
                 for d in out_copies(t - 1):
                     d.start()
 
-    for d in out_copies(nt - 1):
-        d.start()
+        @pl.when(is_kind(i, ("own",)))
+        def _():
+            @pl.when(t == 0)
+            def _():
+                for d in out_copies(nt - 1):
+                    d.start()
+
+            h = jnp.concatenate([hn[3, rows, :], w1b[0, rows, :W]], axis=1)
+            total = acc[rows, :cols] + jnp.dot(h, w2c[3, :, :, :, :cols].reshape(4 * HW, cols), preferred_element_type=f32)
+            y_out[pl.ds(pl.multiple_of(c * tok + t * TT, TT), TT), :] = total.astype(BF)
+
     for cp in copies.values():
         cp().wait_send()
     for t in range(nt):

time: 366 us -> 362 us (0.989)
  no operation moved by 1% of the time
where the time goes in v4:
time: 362 us
  Pallas kernels  360 us (99%)
    pallas_call x1, Pallas kernels, local_mlp(): pl.pallas_call(kernel, out_shape=[pltpu.VMEM(x_blk.shape, BF), jax.ShapeD...  360 us

profile of v4, /device:TPU:0, one launch (start us, length us, event | category | flops | bytes accessed | tf_op | source)
XLA Modules:
  0.0 362.4 jit_solution(2127408061711734356)
XLA Ops:
  0.0 359.6 %shard_map.37 = (bf16[4096,768]{1,0:T(8,128)(2,1)S(1)}, bf16[1536,2048]{1,0:T(8,128)(2,1)}, bf16[8,1536,256]{2,1,0:T(8,128)(2,1)}, bf16[8,1536,256]{2,1,0:T(8,12...) custom-call(bf16[4096,768]{1,0:T(8,128)(2,1)} %x_in.1, ...), custom_call_target="tpu_custom_call" | custom-call | tf_op jit(solution)/shard_map/pallas_call | solution.py:417
  359.6 2.7 copy.5

commit v5 on v4

--- a/solution.py
+++ b/solution.py
@@ -24,8 +24,8 @@
     ("hid", 0, 6, 3, 4), ("full", 0, 4, 0, 1), ("full", 1, 5, 0, 4), ("full", 0, 0, 0, 4),
     ("full", 1, 4, 2, 4), ("full", 1, 4, 0, 1), ("full", 0, 2, 0, 4), ("full", 1, 3, 0, 4),
     ("full", 1, 4, 1, 2), ("full", 1, 2, 0, 4), ("full", 1, 0, 0, 4), ("part", 1, 6, 0, 4),
-    ("full", 1, 1, 0, 4), ("part", 1, 7, 0, 4), ("comp", 1, 0, 0, 4), ("comp", 1, 1, 0, 4),
-    ("comp", 1, 2, 0, 4), ("last", 1, 3, 0, 4), ("own", 1, 3, 0, 4),
+    ("full", 1, 1, 0, 4), ("part", 1, 7, 0, 4), ("six", 1, 6, 0, 4), ("comp", 1, 2, 0, 4),
+    ("last", 1, 3, 0, 4), ("own", 1, 3, 0, 4),
 )
 LINK_X = (
     "Xx1", "Xx2", "Xz0", "Xz2", "Xz1", "Xx0", "Xz3", "D5", "Xx3", "A5", "D4", "D3",
@@ -74,26 +74,15 @@
     58: ("D7",),
     59: ("L21",),
     60: ("Q0",),
-    62: ("Q1",),
-    64: ("P1",),
-    68: ("Q2",),
-    69: ("P2",),
-    74: ("P3", "Q3",),
+    61: ("Q1", "P1"),
+    67: ("Q2", "P2"),
+    70: ("P3", "Q3"),
 }
 NT = 4
 TILES = [(i, t) for i, s in enumerate(STEPS) for t in range(s[3], s[4])]
 N_TILES = len(TILES)
 FIRST = [TILES.index((i, s[3])) for i, s in enumerate(STEPS)]
 NEW_X = [min(b for b in range(N_TILES) if TILES[b][1] == t) for t in range(NT)]
-
-
-def step_and_tile(b):
-    i = off = jnp.int32(0)
-    for n in range(1, len(STEPS)):
-        begun = (b >= FIRST[n]).astype(jnp.int32)
-        i += begun
-        off += begun * ((FIRST[n] - STEPS[n][3]) - (FIRST[n - 1] - STEPS[n - 1][3]))
-    return i, b + STEPS[0][3] - off
 
 
 def links_after():
@@ -242,7 +231,7 @@
 
     def load(i):
         kind, far, k = STEPS[i][:3]
-        if kind in ("comp", "last", "own"):
+        if kind in ("six", "comp", "last", "own"):
             return
         need = [f"fD{k}" if far else f"fY{k}"]
         if kind == "full":
@@ -265,7 +254,9 @@
         kind, _, k = STEPS[i][:3]
         if kind in ("comp", "last"):
             got(f"fP{k}", f"fQ{k}")
-        if kind in ("comp", "last", "own"):
+        if kind == "six":
+            got("fP0", "fQ0", "fP1", "fQ1")
+        if kind in ("six", "comp", "last", "own"):
             return
         for d in w1_loads(i) + (w2_loads(i, w2, w2s) if kind == "full" else []):
             pltpu.make_async_copy(*d).wait()
@@ -316,18 +307,18 @@
     @pl.loop(0, N_TILES)
     def _(b):
         def pick(lo, hi):
-            if not any(n in busy for n in range(lo, hi)):
-                return lambda: None
             if hi - lo == 1:
-                return functools.partial(before, lo)
+                def leaf():
+                    if lo in busy:
+                        before(lo)
+                    return tuple(jnp.int32(v) for v in TILES[lo])
+                return leaf
             mid = (lo + hi) // 2
             low, high = pick(lo, mid), pick(mid, hi)
             return lambda: lax.cond(b < mid, low, high)
 
         busy = set(HOOKS) | set(FIRST) | set(NEW_X)
-        pick(0, N_TILES)()
-
-        i, t = step_and_tile(b)
+        i, t = pick(0, N_TILES)()
         slot = lax.rem(i, 2)
         rows = at(t, TT, TT)
 
@@ -363,9 +354,21 @@
         def down(j, half, lo, hi):
             return w2c[j, half, :, :, lo * cols:hi * cols].reshape(2 * HW, (hi - lo) * cols)
 
+        @pl.when(is_kind(i, ("six",)))
+        def _():
+            both = range(2)
+            ps = [jnp.dot(xs[r, at(1 - y, dh)], jnp.concatenate([wl[j] for j in both], axis=1), preferred_element_type=f32)
+                  for r in subs]
+            for r, p in zip(subs, ps):
+                hs = []
+                for j in both:
+                    hs += [hn[j, r, :], gelu(p32[j, r, :] + p[:, j * W:(j + 1) * W]).astype(BF)]
+                v = w2c[0:2].reshape(8 * HW, 2 * cols)
+                acc[r, :] += jnp.dot(jnp.concatenate(hs, axis=1), v, preferred_element_type=f32)
+
         @pl.when(is_kind(i, ("comp",)))
         def _():
-            j = i - STEPS.index(("comp", 1, 0, 0, NT))
+            j = 2
             for r, p in zip(subs, far_p(j)):
                 total = acc[r, :] + jnp.dot(hn[j, r, :], down(j, 0, 0, 2), preferred_element_type=f32)
                 acc[r, :] = total + jnp.dot(gelu(p).astype(BF), down(j, 1, 0, 2), preferred_element_type=f32)

time: 362 us -> 362 us (level)
  no operation moved by 1% of the time
where the time goes in v5:
time: 362 us; the launch traced here: 361 us
  Pallas kernels  359 us (99%)
    pallas_call x1, Pallas kernels, local_mlp(): pl.pallas_call(kernel, out_shape=[pltpu.VMEM(x_blk.shape, BF), jax.ShapeD...  359 us

profile of v5, /device:TPU:0, one launch (start us, length us, event | category | flops | bytes accessed | tf_op | source)
XLA Modules:
  0.0 361.4 jit_solution(18145557619721250587)
XLA Ops:
  0.0 358.7 %shard_map.37 = (bf16[4096,768]{1,0:T(8,128)(2,1)S(1)}, bf16[1536,2048]{1,0:T(8,128)(2,1)}, bf16[8,1536,256]{2,1,0:T(8,128)(2,1)}, bf16[8,1536,256]{2,1,0:T(8,12...) custom-call(bf16[4096,768]{1,0:T(8,128)(2,1)} %x_in.1, ...), custom_call_target="tpu_custom_call" | custom-call | tf_op jit(solution)/shard_map/pallas_call | solution.py:420
  358.7 2.7 copy.5
